TPU v7x, 32 devices: a whole 2x2x4 slice. The times are simulated.
32 devices in a mesh: gx: 8 (over z, core), gz: 4 (over y, x).
Axes of the slice: x: 2, y: 2, z: 4, core: 2. Of those that a mesh axis runs over, the one named last changes fastest.
Arguments:
- view_index: int32 [1], replicated, may hold values from 0 to 5
- psf_taps: float32 [6, 3, 31], replicated, may hold values from 0.1 to 1
- extents: int32 [6, 3], replicated, may hold values from 4 to 15
- estimate: float32 [16, 256, 1024], P(None, 'gz', 'gx'), may hold values from 0.5 to 2
- measured: float32 [16, 256, 1024], P(None, 'gz', 'gx'), may hold values from 0.25 to 4
Outputs:
- upsampled: float32 [16, 1024, 1024], P('gz', None, 'gx')
All inputs are finite; a program needn't handle non-finite values.
Results may differ from a plain program's by a relative error of at most 0.004.
Values may be sent and summed in bfloat16 or wider, within the bound.
A program may use at most 64 MiB of HBM per device.

v0:
```python
import math

import jax
import jax.numpy as jnp
from jax import lax
from jax.sharding import PartitionSpec as P

HALF = 15
TAPS = 31
UP = 4


def extended(cells, sides, width):
    for axis, dim in sides:
        count = lax.axis_size(axis)
        ends = count - 1
        head = lax.slice_in_dim(cells, 0, width, axis=dim)
        tail = lax.slice_in_dim(cells, cells.shape[dim] - width, cells.shape[dim], axis=dim)
        cells = jnp.concatenate(
            [
                lax.ppermute(tail, axis, [(i, (i + 1) % count) for i in range(ends)]),
                cells,
                lax.ppermute(head, axis, [((i + 1) % count, i) for i in range(ends)]),
            ],
            axis=dim,
        )
    return cells


def pick_kernels(view_index, psf_taps, extents):
    selector = (jnp.arange(psf_taps.shape[0], dtype=jnp.int32) == view_index[0]).astype(jnp.float32)
    picked = jnp.sum(psf_taps * selector[:, None, None], axis=0)
    reach = jnp.sum(extents.astype(jnp.float32) * selector[:, None], axis=0)
    offsets = (jnp.arange(TAPS, dtype=jnp.int32) - HALF).astype(jnp.float32)
    kernels = []
    for axis_id in range(3):
        unnormalized_taps = picked[axis_id] * (jnp.abs(offsets) <= reach[axis_id]).astype(
            jnp.float32
        )
        kernels.append(unnormalized_taps / jnp.sum(unnormalized_taps))
    return kernels


def smear_valid(padded, kernel, axis_dim):
    length = padded.shape[axis_dim] - 2 * HALF
    total = jnp.zeros(
        padded.shape[:axis_dim] + (length,) + padded.shape[axis_dim + 1 :], jnp.float32
    )
    for tap_index in range(TAPS):
        total = total + kernel[tap_index] * lax.slice_in_dim(
            padded, tap_index, tap_index + length, axis=axis_dim
        )
    return total


def local_convolve(volume, kernel, axis_dim):
    pad_widths = [(0, 0), (0, 0), (0, 0)]
    pad_widths[axis_dim] = (HALF, HALF)
    return smear_valid(jnp.pad(volume, pad_widths), kernel, axis_dim)


def blur(volume, kernels):
    wide = extended(volume, (("gx", 2),), HALF)
    section_one = smear_valid(wide, kernels[0], 2)
    section_two = local_convolve(section_one, kernels[1], 0)
    tall = extended(section_two, (("gz", 1),), HALF)
    return smear_valid(tall, kernels[2], 1)


def build_table(first_row, count_of_rows, length):
    row_ids = first_row + jnp.arange(count_of_rows, dtype=jnp.int32)[:, None]
    column_numbers = jnp.arange(length, dtype=jnp.int32)[None, :]
    offset_units = jnp.mod(row_ids - UP * column_numbers, UP * length)
    sine_part = jnp.sin(jnp.pi * jnp.mod(offset_units, 2 * UP).astype(jnp.float32) / UP)
    tangent_part = length * jnp.tan(jnp.pi * offset_units.astype(jnp.float32) / (UP * length))
    on_grid = jnp.mod(offset_units, UP) == 0
    guarded_denominator = jnp.where(on_grid, jnp.float32(1.0), tangent_part)
    entries = jnp.where(
        on_grid,
        jnp.where(offset_units == 0, jnp.float32(1.0), jnp.float32(0.0)),
        sine_part / guarded_denominator,
    )
    return entries.astype(jnp.bfloat16)


def upsample(depth_columns):
    length = depth_columns.shape[1]
    rows_out = length * UP
    block_rows = math.gcd(rows_out, 512)
    block_count = rows_out // block_rows

    def block_out(block_index):
        slab_lookup_table = build_table(block_index * block_rows, block_rows, length)
        return jnp.einsum(
            "ep,hps->hes", slab_lookup_table, depth_columns, preferred_element_type=jnp.float32
        )

    pieces = lax.map(block_out, jnp.arange(block_count, dtype=jnp.int32))
    return jnp.transpose(pieces, (1, 0, 2, 3)).reshape(
        depth_columns.shape[0], rows_out, depth_columns.shape[2]
    )


def on_device(view_index, psf_taps, extents, estimate, measured):
    kernels = pick_kernels(view_index, psf_taps, extents)
    adjoint_direction = [kernel[::-1] for kernel in kernels]
    blurred = blur(estimate, kernels)
    quotient = measured / blurred
    correction = blur(quotient, adjoint_direction)
    rounded = (estimate * correction).astype(jnp.bfloat16)
    return upsample(lax.all_to_all(rounded, "gz", split_axis=0, concat_axis=1, tiled=True))


def solution(mesh):
    return jax.shard_map(
        on_device,
        mesh=mesh,
        in_specs=(P(), P(), P(), P(None, "gz", "gx"), P(None, "gz", "gx")),
        out_specs=P("gz", None, "gx"),
        check_vma=False,
    )
```

profile of v0, /device:TPU:8, one launch (start us, length us, event | category | flops | bytes accessed | tf_op | source)
XLA Modules:
  0.0 214.4 jit_solution(3570523419888991835)
XLA Ops:
  0.0 2.2 %fusion.490 = (f32[16,64,15]{2,1,0:T(8,128)}, f32[16,64,15]{2,1,0:T(8,128)S(1)}) fusion(f32[16,64,128]{2,1,0:T(8,128)} %param.10), kind=kLoop, calls=%fused_computation.795 | loop fusion | bytes 245760 | tf_op jit(solution)/shard_map/slice | solution.py:17
  2.2 1.9 collective-permute-start.1
  4.1 2.4 %collective-permute-start = (f32[16,64,15]{2,1,0:T(8,128)S(1)}, f32[16,64,15]{2,1,0:T(8,128)S(1)}, u32[]{:S(2)}, u32[]{:S(2)}) collective-permute-start(f32[16,64,15]{2,1,0:T(8,128)S(1)} %get-tuple-element.110), channel_id=1, source_target_pairs={{0,4},{4,8},{8,12},{12,16},{16,20},{20,24},{24,28},{1,5},{5,9},{9,... | collective-permute-start | bytes 184328 | tf_op jit(solution)/shard_map/ppermute | solution.py:21
  8.1 2.6 %fusion.484 = (f32[]{:T(128)}, f32[31]{0:T(128)S(1)}, f32[]{:T(128)}, f32[31]{0:T(128)S(1)}, f32[]{:T(128)}, /*index=5*/f32[31]{0:T(128)S(1)}) fusion(f32[3,31]{1,0:T(4,128)S(1)} %multiply_reduce_fusion, f32[]{:T(128)} %bitcast.5, f32[]{:T(128)} %bitcast.11, f32[]{:T(128)} %bitcast.8), kind=kLoop, calls=%fused_computation.789 | loop fusion | flops 369 | bytes 768 | tf_op jit(solution)/shard_map/reduce_sum | solution.py:40
  13.6 0.7 fusion.500
  15.7 0.7 fusion.497
  16.4 0.7 fusion.495
  17.9 25.3 %fusion.318 = f32[16,64,128]{2,1,0:T(8,128)S(1)} fusion(f32[16,64,15]{2,1,0:T(8,128)S(1)} %collective-permute-done, f32[16,64,128]{2,1,0:T(8,128)S(1)} %copy-done, f32[16,64,143]{2,1,0:T(8,128)S(1)} %constant_dynamic-update-slice_fusion, f32[]{:T(128)} %bitcast.46, f32[]{:T(128)} %bitcast.45, f32[]{:T(128)} %bitcast.44, f32[]{:T(128)} %bitcast.43, ...), kind=kLoop, calls=%fused_computation.586 | loop fusion | flops 9961472 | bytes 8974460 | tf_op jit(solution)/shard_map/add | solution.py:50
  43.3 20.5 %fusion.408 = f32[16,64,128]{2,1,0:T(8,128)S(1)} fusion(f32[16,64,128]{2,1,0:T(8,128)S(1)} %fusion.318, f32[]{:T(128)} %bitcast.76, f32[]{:T(128)} %bitcast.75, f32[]{:T(128)} %bitcast.74, f32[]{:T(128)} %bitcast.73, f32[]{:T(128)} %bitcast.72, f32[]{:T(128)} %bitcast.71, f32[]{:T(128)} %bitcast.70, f32[]{:T(128)} %bitcast.69, f32[]{:T(128)} %bitcast.68, ...), kind=kLoop, calls=%fused_computation.676 | loop fusion | flops 7995392 | bytes 1048700 | tf_op jit(solution)/shard_map/add | solution.py:50
  63.9 3.4 %collective-permute-start.2 = (f32[16,15,128]{2,1,0:T(8,128)S(1)}, f32[16,15,128]{2,1,0:T(8,128)S(1)}, u32[]{:S(2)}, u32[]{:S(2)}) collective-permute-start(f32[16,15,128]{2,1,0:T(8,128)S(1)} %get-tuple-element.107), channel_id=1, source_target_pairs={{0,1},{1,2},{2,3},{4,5},{5,6},{6,7},{8,9},{9,10},{10,11},{12,13},{... | collective-permute-start | bytes 368648 | tf_op jit(solution)/shard_map/ppermute | solution.py:21
  67.3 1.3 collective-permute-start.3
  69.3 0.7 fusion.493
  70.0 0.9 collective-permute-done.2
  70.9 4.8 %collective-permute-done.3 = f32[16,15,128]{2,1,0:T(8,128)S(1)} collective-permute-done((f32[16,15,128]{2,1,0:T(8,128)S(1)}, f32[16,15,128]{2,1,0:T(8,128)S(1)}, u32[]{:S(2)}, u32[]{:S(2)}) %collective-permute-start.3) | collective-permute-done | bytes 122912 | tf_op jit(solution)/shard_map/ppermute | solution.py:23
  75.7 21.7 %fusion.130 = f32[16,64,128]{2,1,0:T(8,128)S(1)} fusion(f32[16,64,128]{2,1,0:T(8,128)S(1)} %copy-done.1, f32[16,64,128]{2,1,0:T(8,128)S(1)} %fusion.408, f32[16,15,128]{2,1,0:T(8,128)S(1)} %collective-permute-done.3, f32[16,15,128]{2,1,0:T(8,128)S(1)} %collective-permute-done.2, f32[]{:T(128)} %bitcast.106, f32[]{:T(128)} %bitcast.105, f32[]{:T(128)} %bitcast.104, ...), kind=kLoop, calls=%fused_computation.398 | loop fusion | flops 12058624 | bytes 1818748 | tf_op jit(solution)/shard_map/div | solution.py:108
  97.6 2.0 collective-permute-start.4
  99.6 3.5 %collective-permute-start.5 = (f32[16,64,15]{2,1,0:T(8,128)S(1)}, f32[16,64,15]{2,1,0:T(8,128)S(1)}, u32[]{:S(2)}, u32[]{:S(2)}) collective-permute-start(f32[16,64,15]{2,1,0:T(8,128)S(1)} %get-tuple-element.106), channel_id=1, source_target_pairs={{4,0},{8,4},{12,8},{16,12},{20,16},{24,20},{28,24},{5,1},{9,5},{13... | collective-permute-start | bytes 184328 | tf_op jit(solution)/shard_map/ppermute | solution.py:23
  103.9 4.2 %collective-permute-done.4 = f32[16,64,15]{2,1,0:T(8,128)S(1)} collective-permute-done((f32[16,64,15]{2,1,0:T(8,128)S(1)}, f32[16,64,15]{2,1,0:T(8,128)S(1)}, u32[]{:S(2)}, u32[]{:S(2)}) %collective-permute-start.4) | collective-permute-done | bytes 61472 | tf_op jit(solution)/shard_map/ppermute | solution.py:21
  108.1 1.8 collective-permute-done.5
  109.9 27.7 %fusion.216 = f32[16,64,128]{2,1,0:T(8,128)S(1)} fusion(f32[16,64,128]{2,1,0:T(8,128)S(1)} %fusion.130, f32[16,64,15]{2,1,0:T(8,128)S(1)} %collective-permute-done.5, f32[16,64,15]{2,1,0:T(8,128)S(1)} %collective-permute-done.4, f32[]{:T(128)} %bitcast.136, f32[]{:T(128)} %bitcast.135, f32[]{:T(128)} %bitcast.134, f32[]{:T(128)} %bitcast.133, f32[]{:T(128)} %bitcast.132, ...), kind=kLoop, calls=%fused_computation.484 | loop fusion | flops 11927552 | bytes 1171580 | tf_op jit(solution)/shard_map/add | solution.py:50
  137.5 20.2 %fusion.468 = f32[16,64,128]{2,1,0:T(8,128)S(1)} fusion(f32[16,64,128]{2,1,0:T(8,128)S(1)} %fusion.216, f32[]{:T(128)} %bitcast.166, f32[]{:T(128)} %bitcast.165, f32[]{:T(128)} %bitcast.164, f32[]{:T(128)} %bitcast.163, f32[]{:T(128)} %bitcast.162, f32[]{:T(128)} %bitcast.161, f32[]{:T(128)} %bitcast.160, f32[]{:T(128)} %bitcast.159, f32[]{:T(128)} %bitcast.158, ...), kind=kLoop, calls=%fused_computation.736 | loop fusion | flops 7995392 | bytes 1048700 | tf_op jit(solution)/shard_map/add | solution.py:50
  157.8 4.1 %collective-permute-start.6 = (f32[16,15,128]{2,1,0:T(8,128)S(1)}, f32[16,15,128]{2,1,0:T(8,128)S(1)}, u32[]{:S(2)}, u32[]{:S(2)}) collective-permute-start(f32[16,15,128]{2,1,0:T(8,128)S(1)} %get-tuple-element.103), channel_id=1, source_target_pairs={{0,1},{1,2},{2,3},{4,5},{5,6},{6,7},{8,9},{9,10},{10,11},{12,13},{... | collective-permute-start | bytes 368648 | tf_op jit(solution)/shard_map/ppermute | solution.py:21
  161.9 1.5 collective-permute-start.7
  164.1 0.7 fusion.491
  164.9 4.7 %collective-permute-done.7 = f32[16,15,128]{2,1,0:T(8,128)S(1)} collective-permute-done((f32[16,15,128]{2,1,0:T(8,128)S(1)}, f32[16,15,128]{2,1,0:T(8,128)S(1)}, u32[]{:S(2)}, u32[]{:S(2)}) %collective-permute-start.7) | collective-permute-done | bytes 122912 | tf_op jit(solution)/shard_map/ppermute | solution.py:23
  169.6 22.4 %fusion.43 = bf16[16,64,128]{2,1,0:T(8,128)(2,1)} fusion(f32[16,64,128]{2,1,0:T(8,128)S(1)} %copy-done, f32[16,64,128]{2,1,0:T(8,128)S(1)} %fusion.468, f32[16,15,128]{2,1,0:T(8,128)S(1)} %collective-permute-done.7, f32[16,15,128]{2,1,0:T(8,128)S(1)} %collective-permute-done.6, f32[]{:T(128)} %bitcast.196, f32[]{:T(128)} %bitcast.195, f32[]{:T(128)} %bitcast.194, ...), kind=kLoop, calls=%fused_computation.311 | loop fusion | flops 12189696 | bytes 1556604 | tf_op jit(solution)/shard_map/convert_element_type | solution.py:110
  192.0 3.4 %all-to-all-start = ((bf16[16,64,128]{2,1,0:T(8,128)(2,1)}), bf16[16,64,128]{2,1,0:T(8,128)(2,1)S(1)}, u32[]{:S(2)}, u32[]{:S(2)}) async-start(bf16[16,64,128]{2,1,0:T(8,128)(2,1)} %fusion.43), calls=%async_computation | async-start | bytes 524288 | tf_op jit(solution)/shard_map/all_to_all | solution.py:111
  195.4 6.0 %all-to-all-done = bf16[16,64,128]{2,1,0:T(8,128)(2,1)S(1)} async-done(((bf16[16,64,128]{2,1,0:T(8,128)(2,1)}), bf16[16,64,128]{2,1,0:T(8,128)(2,1)S(1)}, u32[]{:S(2)}, u32[]{:S(2)}) %all-to-all-start) | async-done | bytes 262176 | tf_op jit(solution)/shard_map/all_to_all | solution.py:111
  201.5 11.4 %while.13 = (s32[]{:T(128)}, f32[2,4,512,128]{3,2,1,0:T(8,128)S(1)}, s32[2]{0:T(128)S(1)}, bf16[4,256,128]{2,1,0:T(8,128)(2,1)S(1)}, s32[]{:T(128)}, /*index=5*/s32[1]{0:T(128)}) while((s32[]{:T(128)}, f32[2,4,512,128]{3,2,1,0:T(8,128)S(1)}, s32[2]{0:T(128)S(1)}, bf16[4,256,128]{2,1,0:T(8,128)(2,1)S(1)}, s32[]{:T(128)}, ...), condition=%wide.region_6.7_spmd, body=%wide.region_5.6_spmd.sunk | while | flops 139854592 | bytes 1316965 | solution.py:98
  202.8 4.4 %fusion.510 = f32[2,4,512,128]{3,2,1,0:T(8,128)S(1)} fusion(f32[2,4,512,128]{3,2,1,0:T(8,128)S(1)} %get-tuple-element.342, s32[]{:T(128)} %get-tuple-element.341, bf16[4,256,128]{2,1,0:T(8,128)(2,1)S(1)} %get-tuple-element.350, s32[256]{0:T(256)S(1)} %iota_multiply_fusion.2, s32[512]{0:T(512)S(1)} %iota_add_fusion.2), kind=kOutput, calls=%fused_computation.1.clone.1 | convolution fusion | flops 139853824 | bytes 1313796 | tf_op jit(solution)/shard_map/while/body/eval_jaxpr/ep,hps->hes/dot_general | solution.py:94
  208.5 4.4 %fusion.510 = f32[2,4,512,128]{3,2,1,0:T(8,128)S(1)} fusion(f32[2,4,512,128]{3,2,1,0:T(8,128)S(1)} %get-tuple-element.342, s32[]{:T(128)} %get-tuple-element.341, bf16[4,256,128]{2,1,0:T(8,128)(2,1)S(1)} %get-tuple-element.350, s32[256]{0:T(256)S(1)} %iota_multiply_fusion.2, s32[512]{0:T(512)S(1)} %iota_add_fusion.2), kind=kOutput, calls=%fused_computation.1.clone.1 | convolution fusion | flops 139853824 | bytes 1313796 | tf_op jit(solution)/shard_map/while/body/eval_jaxpr/ep,hps->hes/dot_general | solution.py:94
  212.9 1.5 copy.7
  (42 shorter events, 9.6 us)
Async XLA Ops:
  0.0 12.8 %copy-start = (f32[16,64,128]{2,1,0:T(8,128)S(1)}, f32[16,64,128]{2,1,0:T(8,128)}, u32[]{:S(2)}) copy-start(f32[16,64,128]{2,1,0:T(8,128)} %param.10) | copy-start | bytes 1572868
  0.0 7.2 %copy-start.3 = (s32[6,3]{0,1:T(4,128)S(1)}, s32[6,3]{0,1:T(4,128)}, u32[]{:S(2)}) copy-start(s32[6,3]{0,1:T(4,128)} %param.9) | copy-start | bytes 220
  0.0 8.0 %copy-start.2 = (f32[6,3,31]{2,1,0:T(4,128)S(1)}, f32[6,3,31]{2,1,0:T(4,128)}, u32[]{:S(2)}) copy-start(f32[6,3,31]{2,1,0:T(4,128)} %param.8) | copy-start | bytes 6700
  2.2 15.6 %collective-permute-start.1 = (f32[16,64,15]{2,1,0:T(8,128)}, f32[16,64,15]{2,1,0:T(8,128)S(1)}, u32[]{:S(2)}, u32[]{:S(2)}) collective-permute-start(f32[16,64,15]{2,1,0:T(8,128)} %get-tuple-element.109), channel_id=1, source_target_pairs={{4,0},{8,4},{12,8},{16,12},{20,16},{24,20},{28,24},{5,1},{9,5},{13... | collective-permute-start | bytes 184328 | tf_op jit(solution)/shard_map/ppermute | solution.py:23
  4.1 13.8 %collective-permute-start = (f32[16,64,15]{2,1,0:T(8,128)S(1)}, f32[16,64,15]{2,1,0:T(8,128)S(1)}, u32[]{:S(2)}, u32[]{:S(2)}) collective-permute-start(f32[16,64,15]{2,1,0:T(8,128)S(1)} %get-tuple-element.110), channel_id=1, source_target_pairs={{0,4},{4,8},{8,12},{12,16},{16,20},{20,24},{24,28},{1,5},{5,9},{9,... | collective-permute-start | bytes 184328 | tf_op jit(solution)/shard_map/ppermute | solution.py:21
  43.3 32.4 %copy-start.1 = (f32[16,64,128]{2,1,0:T(8,128)S(1)}, f32[16,64,128]{2,1,0:T(8,128)}, u32[]{:S(2)}) copy-start(f32[16,64,128]{2,1,0:T(8,128)} %param.11) | copy-start | bytes 1572868
  63.9 7.1 %collective-permute-start.2 = (f32[16,15,128]{2,1,0:T(8,128)S(1)}, f32[16,15,128]{2,1,0:T(8,128)S(1)}, u32[]{:S(2)}, u32[]{:S(2)}) collective-permute-start(f32[16,15,128]{2,1,0:T(8,128)S(1)} %get-tuple-element.107), channel_id=1, source_target_pairs={{0,1},{1,2},{2,3},{4,5},{5,6},{6,7},{8,9},{9,10},{10,11},{12,13},{... | collective-permute-start | bytes 368648 | tf_op jit(solution)/shard_map/ppermute | solution.py:21
  67.3 8.4 %collective-permute-start.3 = (f32[16,15,128]{2,1,0:T(8,128)S(1)}, f32[16,15,128]{2,1,0:T(8,128)S(1)}, u32[]{:S(2)}, u32[]{:S(2)}) collective-permute-start(f32[16,15,128]{2,1,0:T(8,128)S(1)} %get-tuple-element.108), channel_id=1, source_target_pairs={{1,0},{2,1},{3,2},{5,4},{6,5},{7,6},{9,8},{10,9},{11,10},{13,12},{... | collective-permute-start | bytes 368648 | tf_op jit(solution)/shard_map/ppermute | solution.py:23
  97.6 10.5 %collective-permute-start.4 = (f32[16,64,15]{2,1,0:T(8,128)S(1)}, f32[16,64,15]{2,1,0:T(8,128)S(1)}, u32[]{:S(2)}, u32[]{:S(2)}) collective-permute-start(f32[16,64,15]{2,1,0:T(8,128)S(1)} %get-tuple-element.105), channel_id=1, source_target_pairs={{0,4},{4,8},{8,12},{12,16},{16,20},{20,24},{24,28},{1,5},{5,9},{9,... | collective-permute-start | bytes 184328 | tf_op jit(solution)/shard_map/ppermute | solution.py:21
  99.6 10.2 %collective-permute-start.5 = (f32[16,64,15]{2,1,0:T(8,128)S(1)}, f32[16,64,15]{2,1,0:T(8,128)S(1)}, u32[]{:S(2)}, u32[]{:S(2)}) collective-permute-start(f32[16,64,15]{2,1,0:T(8,128)S(1)} %get-tuple-element.106), channel_id=1, source_target_pairs={{4,0},{8,4},{12,8},{16,12},{20,16},{24,20},{28,24},{5,1},{9,5},{13... | collective-permute-start | bytes 184328 | tf_op jit(solution)/shard_map/ppermute | solution.py:23
  157.8 7.1 %collective-permute-start.6 = (f32[16,15,128]{2,1,0:T(8,128)S(1)}, f32[16,15,128]{2,1,0:T(8,128)S(1)}, u32[]{:S(2)}, u32[]{:S(2)}) collective-permute-start(f32[16,15,128]{2,1,0:T(8,128)S(1)} %get-tuple-element.103), channel_id=1, source_target_pairs={{0,1},{1,2},{2,3},{4,5},{5,6},{6,7},{8,9},{9,10},{10,11},{12,13},{... | collective-permute-start | bytes 368648 | tf_op jit(solution)/shard_map/ppermute | solution.py:21
  161.9 7.7 %collective-permute-start.7 = (f32[16,15,128]{2,1,0:T(8,128)S(1)}, f32[16,15,128]{2,1,0:T(8,128)S(1)}, u32[]{:S(2)}, u32[]{:S(2)}) collective-permute-start(f32[16,15,128]{2,1,0:T(8,128)S(1)} %get-tuple-element.104), channel_id=1, source_target_pairs={{1,0},{2,1},{3,2},{5,4},{6,5},{7,6},{9,8},{10,9},{11,10},{13,12},{... | collective-permute-start | bytes 368648 | tf_op jit(solution)/shard_map/ppermute | solution.py:23
  192.0 9.5 %all-to-all-start = ((bf16[16,64,128]{2,1,0:T(8,128)(2,1)}), bf16[16,64,128]{2,1,0:T(8,128)(2,1)S(1)}, u32[]{:S(2)}, u32[]{:S(2)}) async-start(bf16[16,64,128]{2,1,0:T(8,128)(2,1)} %fusion.43), calls=%async_computation | async-start | bytes 524288 | tf_op jit(solution)/shard_map/all_to_all | solution.py:111
where the time goes:
time: 216 us; the launch traced here: 214 us
  other arithmetic  143 us (66%)
  starting transfers between devices  23.6 us (11%)
  waiting for transfers between devices  22.4 us (10%)
  local copies, waits for them, and re-layouts  14.7 us (7%)
  matrix products  8.88 us (4%)
    add x4, other arithmetic, smear_valid(): total + kernel[tap_index] * lax.slice_in_dim(padded, tap_index, tap_index...  93.8 us
    convert_element_type x1, other arithmetic, on_device(): rounded = (estimate * correction).astype(jnp.bfloat16)  22.4 us
    div x1, other arithmetic, on_device(): quotient = measured / blurred  21.7 us
    ppermute x4, starting transfers between devices, extended(): lax.ppermute(tail, axis, [(i, (i + 1) % count) for i in range(ends)])  11.9 us
    ppermute x4, waiting for transfers between devices, extended(): lax.ppermute(head, axis, [((i + 1) % count, i) for i in range(ends)])  11.2 us
    dot_general x2, matrix products, block_out(): jnp.einsum('ep,hps->hes', slab_lookup_table, depth_columns, preferred_ele...  8.88 us
    slice x12, local copies, waits for them, and re-layouts, smear_valid(): kernel[tap_index]  8.54 us
    ppermute x4, starting transfers between devices, extended(): lax.ppermute(head, axis, [((i + 1) % count, i) for i in range(ends)])  8.21 us
  transfers between devices with their start and end apart: 9, of which 7 were waited for; matrix products, arithmetic and copies ran while one was open for 7% of the time, Pallas kernels for 0%

commit v1 on v0

v1 whole, which is shorter than its diff:
```python
import jax
import jax.numpy as jnp
from jax import lax
from jax.sharding import PartitionSpec as P

UP = 4
BF = jnp.bfloat16


def pick_kernels(view_index, psf_taps, extents):
    half = (psf_taps.shape[2] - 1) // 2
    selector = (jnp.arange(psf_taps.shape[0], dtype=jnp.int32) == view_index[0]).astype(jnp.float32)
    picked = jnp.sum(psf_taps * selector[:, None, None], axis=0)
    reach = jnp.sum(extents.astype(jnp.float32) * selector[:, None], axis=0)
    offsets = (jnp.arange(psf_taps.shape[2], dtype=jnp.int32) - half).astype(jnp.float32)
    raw = picked * (jnp.abs(offsets)[None, :] <= reach[:, None]).astype(jnp.float32)
    return raw / jnp.sum(raw, axis=1, keepdims=True)


def band(kernel, rows, cols, lead, sign):
    half = (kernel.shape[0] - 1) // 2
    i = lax.broadcasted_iota(jnp.int32, (rows, cols), 0) - lead
    j = lax.broadcasted_iota(jnp.int32, (rows, cols), 1)
    t = sign * (i - j) + half
    total = jnp.zeros((rows, cols), jnp.float32)
    for tap in range(kernel.shape[0]):
        total = jnp.where(t == tap, kernel[tap], total)
    return total.astype(BF)


def extended(cells, axis, dim, width):
    count = lax.axis_size(axis)
    ends = count - 1
    head = lax.slice_in_dim(cells, 0, width, axis=dim)
    tail = lax.slice_in_dim(cells, cells.shape[dim] - width, cells.shape[dim], axis=dim)
    return jnp.concatenate(
        [
            lax.ppermute(tail, axis, [(i, i + 1) for i in range(ends)]),
            cells,
            lax.ppermute(head, axis, [(i + 1, i) for i in range(ends)]),
        ],
        axis=dim,
    )


def blur(volume, kernels, sign):
    y, z, x = volume.shape
    half = (kernels.shape[1] - 1) // 2
    lead = half + 1
    wide = extended(volume.astype(BF), "gx", 2, lead)
    kx = band(kernels[0], x + 2 * lead, x, lead, sign)
    ky = band(kernels[1], y, y, 0, sign)
    kz = band(kernels[2], z + 2 * lead, z, lead, sign)
    one = jnp.einsum("yzi,ij->yzj", wide, kx, preferred_element_type=jnp.float32).astype(BF)
    two = jnp.einsum("yzi,yj->jzi", one, ky, preferred_element_type=jnp.float32).astype(BF)
    tall = extended(two, "gz", 1, lead)
    return jnp.einsum("zj,yzi->yji", kz, tall, preferred_element_type=jnp.float32)


def build_table(length):
    rows = UP * length
    row_ids = lax.broadcasted_iota(jnp.int32, (rows, length), 0)
    cols = lax.broadcasted_iota(jnp.int32, (rows, length), 1)
    units = jnp.mod(row_ids - UP * cols, rows)
    sine = jnp.sin(jnp.pi * jnp.mod(units, 2 * UP).astype(jnp.float32) / UP)
    tangent = length * jnp.tan(jnp.pi * units.astype(jnp.float32) / rows)
    on_grid = jnp.mod(units, UP) == 0
    guarded = jnp.where(on_grid, jnp.float32(1.0), tangent)
    hit = jnp.where(units == 0, jnp.float32(1.0), jnp.float32(0.0))
    return jnp.where(on_grid, hit, sine / guarded).astype(BF)


def on_device(view_index, psf_taps, extents, estimate, measured):
    kernels = pick_kernels(view_index, psf_taps, extents)
    blurred = blur(estimate, kernels, 1)
    correction = blur(measured / blurred, kernels, -1)
    rounded = (estimate * correction).astype(BF)
    lines = lax.all_to_all(rounded, "gz", split_axis=0, concat_axis=1, tiled=True)
    table = build_table(lines.shape[1])
    return jnp.einsum("mn,ynx->ymx", table, lines, preferred_element_type=jnp.float32)


def solution(mesh):
    return jax.shard_map(
        on_device,
        mesh=mesh,
        in_specs=(P(), P(), P(), P(None, "gz", "gx"), P(None, "gz", "gx")),
        out_specs=P("gz", None, "gx"),
        check_vma=False,
    )
```

time: 216 us -> 184 us (0.85)
  other arithmetic: 143 us -> 2.3 us
  matrix products: 8.88 us -> 127 us
  local copies, waits for them, and re-layouts: 14.7 us -> 7.11 us
  waiting for transfers between devices: 22.4 us -> 19.5 us
    dot_general x2 -> x5, matrix products: 8.88 us -> 127 us  [the longest x2 78.7 us: blur(): jnp.einsum('yzi,yj->jzi', one, ky, preferred_element_type=jnp.float32)]
    add x6 -> x0, other arithmetic: 93.8 us -> none  [the longest x4 93.8 us: smear_valid(): total + kernel[tap_index] * lax.slice_in_dim(padded, tap_index, tap_index...]
    div x4 -> x1, other arithmetic: 23.5 us -> 0.08 us  [pick_kernels(): return raw / jnp.sum(raw, axis=1, keepdims=True)]
    convert_element_type x1 -> x0, other arithmetic: 22.4 us -> none  [on_device(): rounded = (estimate * correction).astype(jnp.bfloat16)]
    slice x14 -> x5, local copies, waits for them, and re-layouts: 11.4 us -> 3.62 us  [band(): total = jnp.where(t == tap, kernel[tap], total)]
    ppermute x8, waiting for transfers between devices: 16.4 us -> 13.7 us  [the longest x4 10.4 us: extended(): lax.ppermute(head, axis, [(i + 1, i) for i in range(ends)])]
    reduce_sum x1, other arithmetic: 2.58 us -> 0.18 us  [pick_kernels(): return raw / jnp.sum(raw, axis=1, keepdims=True)]
  transfers between devices with their start and end apart: 9 -> 9, of which waited for: 7 -> 7; matrix products, arithmetic and copies ran while one was open for 7% -> 3% of each run, Pallas kernels for 0% -> 0%
where the time goes in v1:
time: 184 us; the launch traced here: 182 us
  matrix products  127 us (69%)
  starting transfers between devices  25 us (14%)
  waiting for transfers between devices  19.5 us (11%)
  local copies, waits for them, and re-layouts  7.11 us (4%)
  other arithmetic  2.3 us (1%)
    dot_general x2, matrix products, blur(): jnp.einsum('yzi,yj->jzi', one, ky, preferred_element_type=jnp.float32)  78.7 us
    dot_general x2, matrix products, blur(): jnp.einsum('zj,yzi->yji', kz, tall, preferred_element_type=jnp.float32)  40 us
    ppermute x4, starting transfers between devices, extended(): lax.ppermute(tail, axis, [(i, i + 1) for i in range(ends)])  11.5 us
    ppermute x4, waiting for transfers between devices, extended(): lax.ppermute(head, axis, [(i + 1, i) for i in range(ends)])  10.4 us
    ppermute x4, starting transfers between devices, extended(): lax.ppermute(head, axis, [(i + 1, i) for i in range(ends)])  9.87 us
    dot_general x1, matrix products, on_device(): jnp.einsum('mn,ynx->ymx', table, lines, preferred_element_type=jnp.float32)  8.79 us
    all_to_all x1, waiting for transfers between devices, on_device(): lax.all_to_all(rounded, 'gz', split_axis=0, concat_axis=1, tiled=True)  5.85 us
  transfers between devices with their start and end apart: 9, of which 7 were waited for; matrix products, arithmetic and copies ran while one was open for 3% of the time, Pallas kernels for 0%

profile of v1, /device:TPU:8, one launch (start us, length us, event | category | flops | bytes accessed | tf_op | source)
XLA Modules:
  0.0 182.3 jit_solution(9482646993954202804)
XLA Ops:
  0.0 1.4 copy.31
  1.5 1.9 %collective-permute-start = (bf16[16,64,16]{2,0,1:T(8,128)(2,1)S(1)}, bf16[16,64,16]{2,0,1:T(8,128)(2,1)S(1)}, u32[]{:S(2)}, u32[]{:S(2)}) collective-permute-start(bf16[16,64,16]{2,0,1:T(8,128)(2,1)S(1)} %get-tuple-element.11), channel_id=1, source_target_pairs={{0,4},{4,8},{8,12},{12,16},{16,20},{20,24},{24,28},{1,5},{5,9},{9,... | collective-permute-start | bytes 98312 | tf_op jit(solution)/shard_map/ppermute | solution.py:38
  3.4 3.6 %collective-permute-start.1 = (bf16[16,64,16]{2,0,1:T(8,128)(2,1)S(1)}, bf16[16,64,16]{2,0,1:T(8,128)(2,1)S(1)}, u32[]{:S(2)}, u32[]{:S(2)}) collective-permute-start(bf16[16,64,16]{2,0,1:T(8,128)(2,1)S(1)} %get-tuple-element.12), channel_id=1, source_target_pairs={{4,0},{8,4},{12,8},{16,12},{20,16},{24,20},{28,24},{5,1},{9,5},{13... | collective-permute-start | bytes 98312 | tf_op jit(solution)/shard_map/ppermute | solution.py:40
  7.7 0.8 multiply_reduce_fusion.1
  8.5 0.8 multiply_reduce_fusion
  9.3 0.2 fusion.763
  9.6 0.7 fusion.981
  10.3 0.7 fusion.977
  11.0 0.7 fusion.978
  11.8 0.7 fusion.980
  12.5 0.7 fusion.979
  13.3 39.3 %convolution_convert_fusion.2 = bf16[16,64,128]{2,0,1:T(8,128)(2,1)S(1)} fusion(bf16[16,64,16]{2,0,1:T(8,128)(2,1)S(1)} %collective-permute-done.1, bf16[16,64,128]{2,0,1:T(8,128)(2,1)S(1)} %copy.31, bf16[16,64,16]{2,0,1:T(8,128)(2,1)S(1)} %collective-permute-done, bf16[]{:T(256)} %bitcast.64, bf16[]{:T(256)} %bitcast.63, bf16[]{:T(256)} %bitcast.62, ...), kind=kOutput, calls=%fused_computation.15 | convolution fusion | flops 48709632 | bytes 590588 | tf_op jit(solution)/shard_map/yzi,yj->jzi/dot_general | solution.py:55
  52.6 3.4 %collective-permute-start.2 = (bf16[16,16,128]{2,0,1:T(8,128)(2,1)S(1)}, bf16[16,16,128]{2,0,1:T(8,128)(2,1)S(1)}, u32[]{:S(2)}, u32[]{:S(2)}) collective-permute-start(bf16[16,16,128]{2,0,1:T(8,128)(2,1)S(1)} %get-tuple-element.9), channel_id=1, source_target_pairs={{0,1},{1,2},{2,3},{4,5},{5,6},{6,7},{8,9},{9,10},{10,11},{12,13},{... | collective-permute-start | bytes 196616 | tf_op jit(solution)/shard_map/ppermute | solution.py:38
  56.0 1.3 collective-permute-start.3
  57.3 0.6 collective-permute-done.2
  57.9 4.3 %collective-permute-done.3 = bf16[16,16,128]{2,0,1:T(8,128)(2,1)S(1)} collective-permute-done((bf16[16,16,128]{2,0,1:T(8,128)(2,1)S(1)}, bf16[16,16,128]{2,0,1:T(8,128)(2,1)S(1)}, u32[]{:S(2)}, u32[]{:S(2)}) %collective-permute-start.3) | collective-permute-done | bytes 65568 | tf_op jit(solution)/shard_map/ppermute | solution.py:40
  62.2 19.6 %fusion.3 = bf16[16,64,128]{2,1,0:T(8,128)(2,1)S(1)} fusion(f32[16,64,128]{2,1,0:T(8,128)S(1)} %copy-done.1, bf16[16,96,128]{2,0,1:T(8,128)(2,1)S(1)} %pad_maximum_fusion.1, bf16[]{:T(256)} %bitcast.96, bf16[]{:T(256)} %bitcast.95, bf16[]{:T(256)} %bitcast.94, bf16[]{:T(256)} %bitcast.93, bf16[]{:T(256)} %bitcast.92, bf16[]{:T(256)} %bitcast.91, ...), kind=kOutput, calls=%fused_computation.18 | convolution fusion | flops 25821184 | bytes 1180094 | tf_op jit(solution)/shard_map/zj,yzi->yji/dot_general | solution.py:57
  82.0 1.9 %collective-permute-start.4 = (bf16[16,64,16]{2,1,0:T(8,128)(2,1)S(1)}, bf16[16,64,16]{2,1,0:T(8,128)(2,1)S(1)}, u32[]{:S(2)}, u32[]{:S(2)}) collective-permute-start(bf16[16,64,16]{2,1,0:T(8,128)(2,1)S(1)} %get-tuple-element.7), channel_id=1, source_target_pairs={{0,4},{4,8},{8,12},{12,16},{16,20},{20,24},{24,28},{1,5},{5,9},{9,... | collective-permute-start | bytes 98312 | tf_op jit(solution)/shard_map/ppermute | solution.py:38
  84.0 3.6 %collective-permute-start.5 = (bf16[16,64,16]{2,1,0:T(8,128)(2,1)S(1)}, bf16[16,64,16]{2,1,0:T(8,128)(2,1)S(1)}, u32[]{:S(2)}, u32[]{:S(2)}) collective-permute-start(bf16[16,64,16]{2,1,0:T(8,128)(2,1)S(1)} %get-tuple-element.8), channel_id=1, source_target_pairs={{4,0},{8,4},{12,8},{16,12},{20,16},{24,20},{28,24},{5,1},{9,5},{13... | collective-permute-start | bytes 98312 | tf_op jit(solution)/shard_map/ppermute | solution.py:40
  87.6 2.1 %collective-permute-done.4 = bf16[16,64,16]{2,1,0:T(8,128)(2,1)S(1)} collective-permute-done((bf16[16,64,16]{2,1,0:T(8,128)(2,1)S(1)}, bf16[16,64,16]{2,1,0:T(8,128)(2,1)S(1)}, u32[]{:S(2)}, u32[]{:S(2)}) %collective-permute-start.4) | collective-permute-done | bytes 32800 | tf_op jit(solution)/shard_map/ppermute | solution.py:38
  89.7 1.8 collective-permute-done.5
  91.5 0.3 pad_maximum_fusion
  91.8 39.4 %convolution_convert_fusion = bf16[16,64,128]{2,0,1:T(8,128)(2,1)S(1)} fusion(bf16[16,64,160]{2,1,0:T(8,128)(2,1)S(1)} %pad_maximum_fusion, bf16[]{:T(256)} %bitcast.64, bf16[]{:T(256)} %bitcast.63, bf16[]{:T(256)} %bitcast.62, bf16[]{:T(256)} %bitcast.61, bf16[]{:T(256)} %bitcast.60, bf16[]{:T(256)} %bitcast.59, bf16[]{:T(256)} %bitcast.58, bf16[]{:T(256)} %bitcast.57, ...), kind=kOutput, calls=%fused_computation.13 | convolution fusion | flops 47747328 | bytes 590588 | tf_op jit(solution)/shard_map/yzi,yj->jzi/dot_general | solution.py:55
  131.2 4.3 %collective-permute-start.6 = (bf16[16,16,128]{2,0,1:T(8,128)(2,1)S(1)}, bf16[16,16,128]{2,0,1:T(8,128)(2,1)S(1)}, u32[]{:S(2)}, u32[]{:S(2)}) collective-permute-start(bf16[16,16,128]{2,0,1:T(8,128)(2,1)S(1)} %get-tuple-element.5), channel_id=1, source_target_pairs={{0,1},{1,2},{2,3},{4,5},{5,6},{6,7},{8,9},{9,10},{10,11},{12,13},{... | collective-permute-start | bytes 196616 | tf_op jit(solution)/shard_map/ppermute | solution.py:38
  135.5 1.3 collective-permute-start.7
  136.8 0.6 collective-permute-done.6
  137.4 4.4 %collective-permute-done.7 = bf16[16,16,128]{2,0,1:T(8,128)(2,1)S(1)} collective-permute-done((bf16[16,16,128]{2,0,1:T(8,128)(2,1)S(1)}, bf16[16,16,128]{2,0,1:T(8,128)(2,1)S(1)}, u32[]{:S(2)}, u32[]{:S(2)}) %collective-permute-start.7) | collective-permute-done | bytes 65568 | tf_op jit(solution)/shard_map/ppermute | solution.py:40
  141.9 20.3 %fusion.2 = bf16[16,64,128]{2,1,0:T(8,128)(2,1)} fusion(f32[16,64,128]{2,1,0:T(8,128)S(1)} %copy-done, bf16[16,96,128]{2,0,1:T(8,128)(2,1)S(1)} %pad_maximum_fusion.2, bf16[]{:T(256)} %bitcast.96, bf16[]{:T(256)} %bitcast.95, bf16[]{:T(256)} %bitcast.94, bf16[]{:T(256)} %bitcast.93, bf16[]{:T(256)} %bitcast.92, bf16[]{:T(256)} %bitcast.91, bf16[]{:T(256)} %bitcast.90, ...), kind=kOutput, calls=%fused_computation.17 | convolution fusion | flops 25827328 | bytes 1180094 | tf_op jit(solution)/shard_map/zj,yzi->yji/dot_general | solution.py:57
  162.2 3.6 %all-to-all-start = ((bf16[16,64,128]{2,1,0:T(8,128)(2,1)}), bf16[16,64,128]{2,1,0:T(8,128)(2,1)S(1)}, u32[]{:S(2)}, u32[]{:S(2)}) async-start(bf16[16,64,128]{2,1,0:T(8,128)(2,1)} %fusion.2), calls=%async_computation | async-start | bytes 524288 | tf_op jit(solution)/shard_map/all_to_all | solution.py:78
  165.8 5.8 %all-to-all-done = bf16[16,64,128]{2,1,0:T(8,128)(2,1)S(1)} async-done(((bf16[16,64,128]{2,1,0:T(8,128)(2,1)}), bf16[16,64,128]{2,1,0:T(8,128)(2,1)S(1)}, u32[]{:S(2)}, u32[]{:S(2)}) %all-to-all-start) | async-done | bytes 262176 | tf_op jit(solution)/shard_map/all_to_all | solution.py:78
  171.7 8.8 %convolution_bitcast_fusion = f32[4,1024,128]{1,2,0:T(8,128)S(1)} fusion(bf16[4,256,128]{2,1,0:T(8,128)(2,1)S(1)} %bitcast.138, s32[256]{0:T(256)S(1)} %iota_multiply_fusion), kind=kOutput, calls=%fused_computation | convolution fusion | flops 279707648 | bytes 2360320 | tf_op jit(solution)/shard_map/mn,ynx->ymx/dot_general | solution.py:80
  180.5 1.8 copy.21
  (19 shorter events, 0.5 us)
Async XLA Ops:
  1.5 11.7 %collective-permute-start = (bf16[16,64,16]{2,0,1:T(8,128)(2,1)S(1)}, bf16[16,64,16]{2,0,1:T(8,128)(2,1)S(1)}, u32[]{:S(2)}, u32[]{:S(2)}) collective-permute-start(bf16[16,64,16]{2,0,1:T(8,128)(2,1)S(1)} %get-tuple-element.11), channel_id=1, source_target_pairs={{0,4},{4,8},{8,12},{12,16},{16,20},{20,24},{24,28},{1,5},{5,9},{9,... | collective-permute-start | bytes 98312 | tf_op jit(solution)/shard_map/ppermute | solution.py:38
  3.4 9.8 %collective-permute-start.1 = (bf16[16,64,16]{2,0,1:T(8,128)(2,1)S(1)}, bf16[16,64,16]{2,0,1:T(8,128)(2,1)S(1)}, u32[]{:S(2)}, u32[]{:S(2)}) collective-permute-start(bf16[16,64,16]{2,0,1:T(8,128)(2,1)S(1)} %get-tuple-element.12), channel_id=1, source_target_pairs={{4,0},{8,4},{12,8},{16,12},{20,16},{24,20},{28,24},{5,1},{9,5},{13... | collective-permute-start | bytes 98312 | tf_op jit(solution)/shard_map/ppermute | solution.py:40
  13.2 49.0 %copy-start.1 = (f32[16,64,128]{2,1,0:T(8,128)S(1)}, f32[16,64,128]{2,1,0:T(8,128)}, u32[]{:S(2)}) copy-start(f32[16,64,128]{2,1,0:T(8,128)} %param.9) | copy-start | bytes 1572868
  52.6 5.3 %collective-permute-start.2 = (bf16[16,16,128]{2,0,1:T(8,128)(2,1)S(1)}, bf16[16,16,128]{2,0,1:T(8,128)(2,1)S(1)}, u32[]{:S(2)}, u32[]{:S(2)}) collective-permute-start(bf16[16,16,128]{2,0,1:T(8,128)(2,1)S(1)} %get-tuple-element.9), channel_id=1, source_target_pairs={{0,1},{1,2},{2,3},{4,5},{5,6},{6,7},{8,9},{9,10},{10,11},{12,13},{... | collective-permute-start | bytes 196616 | tf_op jit(solution)/shard_map/ppermute | solution.py:38
  56.0 6.2 %collective-permute-start.3 = (bf16[16,16,128]{2,0,1:T(8,128)(2,1)S(1)}, bf16[16,16,128]{2,0,1:T(8,128)(2,1)S(1)}, u32[]{:S(2)}, u32[]{:S(2)}) collective-permute-start(bf16[16,16,128]{2,0,1:T(8,128)(2,1)S(1)} %get-tuple-element.10), channel_id=1, source_target_pairs={{1,0},{2,1},{3,2},{5,4},{6,5},{7,6},{9,8},{10,9},{11,10},{13,12},{... | collective-permute-start | bytes 196616 | tf_op jit(solution)/shard_map/ppermute | solution.py:40
  82.0 7.7 %collective-permute-start.4 = (bf16[16,64,16]{2,1,0:T(8,128)(2,1)S(1)}, bf16[16,64,16]{2,1,0:T(8,128)(2,1)S(1)}, u32[]{:S(2)}, u32[]{:S(2)}) collective-permute-start(bf16[16,64,16]{2,1,0:T(8,128)(2,1)S(1)} %get-tuple-element.7), channel_id=1, source_target_pairs={{0,4},{4,8},{8,12},{12,16},{16,20},{20,24},{24,28},{1,5},{5,9},{9,... | collective-permute-start | bytes 98312 | tf_op jit(solution)/shard_map/ppermute | solution.py:38
  84.0 7.5 %collective-permute-start.5 = (bf16[16,64,16]{2,1,0:T(8,128)(2,1)S(1)}, bf16[16,64,16]{2,1,0:T(8,128)(2,1)S(1)}, u32[]{:S(2)}, u32[]{:S(2)}) collective-permute-start(bf16[16,64,16]{2,1,0:T(8,128)(2,1)S(1)} %get-tuple-element.8), channel_id=1, source_target_pairs={{4,0},{8,4},{12,8},{16,12},{20,16},{24,20},{28,24},{5,1},{9,5},{13... | collective-permute-start | bytes 98312 | tf_op jit(solution)/shard_map/ppermute | solution.py:40
  91.8 50.0 %copy-start = (f32[16,64,128]{2,1,0:T(8,128)S(1)}, f32[16,64,128]{2,1,0:T(8,128)}, u32[]{:S(2)}) copy-start(f32[16,64,128]{2,1,0:T(8,128)} %param.8) | copy-start | bytes 1572868
  131.2 6.2 %collective-permute-start.6 = (bf16[16,16,128]{2,0,1:T(8,128)(2,1)S(1)}, bf16[16,16,128]{2,0,1:T(8,128)(2,1)S(1)}, u32[]{:S(2)}, u32[]{:S(2)}) collective-permute-start(bf16[16,16,128]{2,0,1:T(8,128)(2,1)S(1)} %get-tuple-element.5), channel_id=1, source_target_pairs={{0,1},{1,2},{2,3},{4,5},{5,6},{6,7},{8,9},{9,10},{10,11},{12,13},{... | collective-permute-start | bytes 196616 | tf_op jit(solution)/shard_map/ppermute | solution.py:38
  135.5 6.3 %collective-permute-start.7 = (bf16[16,16,128]{2,0,1:T(8,128)(2,1)S(1)}, bf16[16,16,128]{2,0,1:T(8,128)(2,1)S(1)}, u32[]{:S(2)}, u32[]{:S(2)}) collective-permute-start(bf16[16,16,128]{2,0,1:T(8,128)(2,1)S(1)} %get-tuple-element.6), channel_id=1, source_target_pairs={{1,0},{2,1},{3,2},{5,4},{6,5},{7,6},{9,8},{10,9},{11,10},{13,12},{... | collective-permute-start | bytes 196616 | tf_op jit(solution)/shard_map/ppermute | solution.py:40
  162.2 9.5 %all-to-all-start = ((bf16[16,64,128]{2,1,0:T(8,128)(2,1)}), bf16[16,64,128]{2,1,0:T(8,128)(2,1)S(1)}, u32[]{:S(2)}, u32[]{:S(2)}) async-start(bf16[16,64,128]{2,1,0:T(8,128)(2,1)} %fusion.2), calls=%async_computation | async-start | bytes 524288 | tf_op jit(solution)/shard_map/all_to_all | solution.py:78
